TPU v7x, 32 devices: a whole 2x2x4 slice. The times are simulated.
32 devices in a mesh: grp: 4 (over y, x), mem: 8 (over z, core).
Axes of the slice: x: 2, y: 2, z: 4, core: 2. Of those that a mesh axis runs over, the one named last changes fastest.
Arguments:
- values: bfloat16 [32, 8, 32, 128], P(('grp', 'mem')), may hold values from -6 to 6
- slots: int32 [32, 8, 32], P(('grp', 'mem')), may hold values from 0 to 7167
- counts: int32 [32, 8], P(('grp', 'mem')), may hold values from 0 to 32, as said below
Outputs:
- averaged: float32 [57344, 128], P('mem')
- returned: bfloat16 [32, 8, 32, 128], P(('grp', 'mem'))
Inputs may be any that keep to these rules, and one draw needn't show every extreme that they name: `counts`: every device has at least one list with exactly 32 valid entries.
All inputs are finite; a program needn't handle non-finite values.
Results may differ from a plain program's by a relative error of at most 0.0024.
Values may be sent and summed in bfloat16 or wider, within the bound.
No kernel may reach another device: no remote copies, remote signals or barrier semaphores. Data moves between devices by JAX's collectives and lax.ppermute only.
A program may use at most 64 MiB of HBM per device.

v0:
```python
import math
import jax
import jax.numpy as jnp
from jax import lax
from jax.sharding import PartitionSpec as P

BUCKET = 7168


def tiled_sums(rows_in, slot_in):
    lane_count = rows_in.shape[1]
    tile = math.gcd(BUCKET, 1024)

    def one_tile(first):
        wanted = first + lax.broadcasted_iota(jnp.int32, (tile, 1), 0)
        onehot = (wanted == slot_in[None, :]).astype(jnp.bfloat16)
        return jnp.dot(onehot, rows_in, preferred_element_type=jnp.float32)

    starts = jnp.arange(BUCKET // tile, dtype=jnp.int32) * tile
    return lax.map(one_tile, starts).reshape(BUCKET, lane_count)


def live_counts(slot_in):
    live_in = (slot_in >= 0).astype(jnp.float32)
    return jax.ops.segment_sum(live_in, jnp.maximum(slot_in, 0), num_segments=BUCKET)


def per_device(values, slots, counts):
    blocks_out = values[0]
    slot_ids = slots[0]
    list_counts = counts[0]
    members, capacity, lane_count = blocks_out.shape
    is_valid = lax.broadcasted_iota(jnp.int32, (members, capacity), 1) < list_counts[:, None]
    send_blocks = jnp.where(is_valid[:, :, None], blocks_out, jnp.zeros_like(blocks_out))
    send_slots = jnp.where(is_valid, slot_ids, -1)
    got_blocks, got_slots = (
        lax.all_to_all(send_blocks, "mem", split_axis=0, concat_axis=0, tiled=True),
        lax.all_to_all(send_slots, "mem", split_axis=0, concat_axis=0, tiled=True),
    )
    rows_in = got_blocks.reshape(members * capacity, lane_count)
    slot_in = got_slots.reshape(members * capacity)
    slot_count = None
    local_sums = tiled_sums(rows_in, slot_in)
    payload = (local_sums, live_counts(slot_in))
    reduced = lax.psum(payload, "grp")
    total_count = reduced[1]
    averaged = reduced[0] / jnp.maximum(total_count, 1.0)[:, None]
    owned_rows = jnp.take(averaged, jnp.maximum(slot_in, 0), axis=0)
    back_rows = jnp.where((slot_in >= 0)[:, None], owned_rows, 0.0).astype(jnp.bfloat16)
    back_rows = back_rows.reshape(members, capacity, lane_count)
    returned = lax.all_to_all(back_rows, "mem", split_axis=0, concat_axis=0, tiled=True)
    return (averaged, returned[None])


def solution(mesh):
    return jax.shard_map(
        per_device,
        mesh=mesh,
        in_specs=(
            P(("grp", "mem"), None, None, None),
            P(("grp", "mem"), None, None),
            P(("grp", "mem"), None),
        ),
        out_specs=(P("mem", None), P(("grp", "mem"), None, None, None)),
        check_vma=False,
    )
```

profile of v0, /device:TPU:0, one launch (start us, length us, event | category | flops | bytes accessed | tf_op | source)
XLA Modules:
  0.0 168.0 jit_solution(9887654835759522025)
XLA Ops:
  7.2 1.4 compare_select_fusion
  8.5 6.4 %all-to-all-start = ((s32[8,1,32]{2,1,0:T(1,128)}), s32[8,1,32]{2,1,0:T(1,128)S(1)}, u32[]{:S(2)}, u32[]{:S(2)}) async-start(s32[8,1,32]{2,1,0:T(1,128)} %compare_select_fusion), calls=%async_computation | async-start | bytes 8192 | tf_op jit(solution)/shard_map/all_to_all | solution.py:38
  14.9 0.7 iota_compare_fusion
  15.6 1.6 bitcast_select_fusion
  17.2 3.2 %all-to-all-done = s32[8,1,32]{2,1,0:T(1,128)S(1)} async-done(((s32[8,1,32]{2,1,0:T(1,128)}), s32[8,1,32]{2,1,0:T(1,128)S(1)}, u32[]{:S(2)}, u32[]{:S(2)}) %all-to-all-start) | async-done | bytes 1056 | tf_op jit(solution)/shard_map/all_to_all | solution.py:38
  20.4 3.4 %all-to-all-start.1 = ((bf16[8,32,128]{2,1,0:T(8,128)(2,1)}), bf16[8,32,128]{2,1,0:T(8,128)(2,1)S(1)}, u32[]{:S(2)}, u32[]{:S(2)}) async-start(bf16[8,32,128]{2,1,0:T(8,128)(2,1)} %bitcast_select_fusion), calls=%async_computation.1 | async-start | bytes 131072 | tf_op jit(solution)/shard_map/all_to_all | solution.py:37
  23.9 5.7 %all-to-all-done.1 = bf16[8,32,128]{2,1,0:T(8,128)(2,1)S(1)} async-done(((bf16[8,32,128]{2,1,0:T(8,128)(2,1)}), bf16[8,32,128]{2,1,0:T(8,128)(2,1)S(1)}, u32[]{:S(2)}, u32[]{:S(2)}) %all-to-all-start.1) | async-done | bytes 65568 | tf_op jit(solution)/shard_map/all_to_all | solution.py:37
  29.6 16.7 %while.11 = (s32[]{:T(128)}, f32[7,1024,128]{2,1,0:T(8,128)}, s32[7]{0:T(128)S(1)}, s32[8,32]{1,0:T(8,128)}, bf16[256,128]{1,0:T(8,128)(2,1)S(1)}, /*index=5*/s32[256]{0:T(256)S(1)}, s32[]{:T(128)}) while((s32[]{:T(128)}, f32[7,1024,128]{2,1,0:T(8,128)}, s32[7]{0:T(128)S(1)}, s32[8,32]{1,0:T(8,128)}, bf16[256,128]{1,0:T(8,128)(2,1)S(1)}, ...), condition=%wide.wide.region_1.2_spmd, body=%wide.wide.region_0.1_spmd.sunk | while | flops 67372032 | bytes 599645 | solution.py:20
  30.2 0.6 iota_add_fusion.3
  30.8 1.2 fusion.16
  32.6 0.6 iota_add_fusion.3
  33.2 1.2 fusion.16
  35.6 1.2 fusion.16
  38.0 1.2 fusion.16
  40.4 1.2 fusion.16
  42.8 1.2 fusion.16
  44.5 0.6 iota_add_fusion.3
  45.2 1.2 fusion.16
  47.2 2.1 %scatter_custom_fusion = f32[7168]{0:T(1024)S(1)} fusion(s32[256]{0:T(256)S(1)} %reshape.145, f32[256]{0:T(256)S(1)} %reshape.147, f32[]{:T(128)} %constant.16.clone.1), kind=kCustom, calls=%fused_computation.14 | custom fusion | flops 256 | bytes 28676 | tf_op jit(solution)/shard_map/scatter-add | solution.py:25
  49.3 17.7 %psum.15 = f32[7168]{0:T(1024)S(1)} all-reduce(f32[7168]{0:T(1024)S(1)} %scatter_custom_fusion), channel_id=1, replica_groups=mesh['grp'=4,'mem'=8] {'grp'}, use_global_device_ids=true, to_apply=%region_4.5 | all-reduce | flops 7168 | bytes 57344 | tf_op jit(solution)/shard_map/psum | solution.py:45
  67.0 74.6 %all-reduce.2.cloned.1.call-done = f32[7168,128]{1,0:T(8,128)} async-done(((f32[7168,128]{1,0:T(8,128)}), f32[7168,128]{1,0:T(8,128)}) %all-reduce.2.cloned.1.call-update) | async-done | bytes 3670032 | tf_op jit(solution)/shard_map/psum | solution.py:45
  141.6 5.7 %broadcast_divide_fusion = f32[7168,128]{1,0:T(8,128)} fusion(f32[7168,128]{1,0:T(8,128)} %all-reduce.2.cloned.1.call-done, f32[7168]{0:T(1024)S(1)} %broadcast_maximum_fusion), kind=kLoop, calls=%fused_computation.8 | loop fusion | flops 917504 | bytes 7368704 | tf_op jit(solution)/shard_map/div | solution.py:47
  147.3 2.8 %gather_fusion = bf16[256,128]{1,0:T(8,128)(2,1)S(1)} fusion(f32[7168,128]{1,0:T(8,128)} %broadcast_divide_fusion, s32[1024]{0:T(1024)S(1)} %pad_clamp_fusion), kind=kCustom, calls=%fused_computation | custom fusion | bytes 132096 | tf_op jit(solution)/shard_map/jit(_take)/gather | solution.py:48
  150.2 10.3 %all_to_all.19 = bf16[8,32,128]{2,1,0:T(8,128)(2,1)S(1)} all-to-all(bf16[8,32,128]{2,1,0:T(8,128)(2,1)S(1)} %select_convert_fusion), channel_id=1, replica_groups=mesh['grp'=4,'mem'=8] {'mem'}, dimensions={0} | all-to-all | bytes 131072 | tf_op jit(solution)/shard_map/all_to_all | solution.py:51
  (29 shorter events, 8.4 us)
Async XLA Ops:
  8.5 11.9 %all-to-all-start = ((s32[8,1,32]{2,1,0:T(1,128)}), s32[8,1,32]{2,1,0:T(1,128)S(1)}, u32[]{:S(2)}, u32[]{:S(2)}) async-start(s32[8,1,32]{2,1,0:T(1,128)} %compare_select_fusion), calls=%async_computation | async-start | bytes 8192 | tf_op jit(solution)/shard_map/all_to_all | solution.py:38
  20.4 9.2 %copy-start = (s32[8,1,32]{2,1,0:T(1,128)}, s32[8,1,32]{2,1,0:T(1,128)S(1)}, u32[]{:S(2)}) copy-start(s32[8,1,32]{2,1,0:T(1,128)S(1)} %all-to-all-done) | copy-start | bytes 3076
  20.4 9.2 %all-to-all-start.1 = ((bf16[8,32,128]{2,1,0:T(8,128)(2,1)}), bf16[8,32,128]{2,1,0:T(8,128)(2,1)S(1)}, u32[]{:S(2)}, u32[]{:S(2)}) async-start(bf16[8,32,128]{2,1,0:T(8,128)(2,1)} %bitcast_select_fusion), calls=%async_computation.1 | async-start | bytes 131072 | tf_op jit(solution)/shard_map/all_to_all | solution.py:37
  23.8 117.8 %all-reduce.2.cloned.1.call-start = ((), (), s32[]{:S(2)}) async-start(), calls=%async_computation.3 | async-start | bytes 7340032 | tf_op jit(solution)/shard_map/psum | solution.py:45
  46.3 0.7 copy-start.1
Sparse Core Ops, SparseCore 0:
  46.5 95.0 all-reduce.1
where the time goes:
time: 169 us; the launch traced here: 168 us
  waiting for transfers between devices  83.5 us (49%)
  blocking collectives  28 us (17%)
  other arithmetic  16.2 us (10%)
  between operations  14.1 us (8%)
  starting transfers between devices  9.75 us (6%)
  local copies, waits for them, and re-layouts  8.35 us (5%)
  matrix products  8.07 us (5%)
    psum x1, waiting for transfers between devices, per_device(): reduced = lax.psum(payload, 'grp')  74.6 us
    psum x1, blocking collectives, per_device(): reduced = lax.psum(payload, 'grp')  17.7 us
    all_to_all x1, blocking collectives, per_device(): lax.all_to_all(back_rows, 'mem', split_axis=0, concat_axis=0, tiled=True)  10.3 us
    dot_general x7, matrix products, one_tile(): return jnp.dot(onehot, rows_in, preferred_element_type=jnp.float32)  8.07 us
    all_to_all x1, starting transfers between devices, per_device(): lax.all_to_all(send_slots, 'mem', split_axis=0, concat_axis=0, tiled=True)  6.35 us
    div x1, other arithmetic, per_device(): averaged = reduced[0] / jnp.maximum(total_count, 1.0)[:, None]  5.72 us
    all_to_all x1, waiting for transfers between devices, per_device(): lax.all_to_all(send_blocks, 'mem', split_axis=0, concat_axis=0, tiled=True)  5.7 us
    add x7, other arithmetic, one_tile(): wanted = first + lax.broadcasted_iota(jnp.int32, (tile, 1), 0)  4.53 us
  transfers between devices with their start and end apart: 3, of which 3 were waited for; matrix products, arithmetic and copies ran while one was open for 3% of the time, Pallas kernels for 0%

commit v1 on v0

--- a/solution.py
+++ b/solution.py
@@ -5,6 +5,38 @@
 from jax.sharding import PartitionSpec as P
 
 BUCKET = 7168
+
+
+def _shape_goods(local_array, dimension_no, z):
+    part_now = local_array.shape
+    seen_now = local_array.reshape(
+        *part_now[:dimension_no], z, part_now[dimension_no] // z, *part_now[dimension_no + 1 :]
+    )
+    return jnp.moveaxis(seen_now, dimension_no, 0)
+
+
+def settle_the_clusters(arr_in, at_axis):
+    found_now = list(arr_in.shape[1:])
+    found_now[at_axis] *= arr_in.shape[0]
+    return jnp.moveaxis(arr_in, 0, at_axis).reshape(found_now)
+
+
+def _shape_body(panel, mesh_ax, field_in, vector):
+    z1 = jax.lax.psum(1, mesh_ax)
+    f_next = jax.lax.axis_index(mesh_ax)
+    n_now, block_out = (z1, f_next)
+    inter = _shape_goods(panel, field_in, n_now)
+    rows = [inter[block_out]]
+    for hop_no in [*range(1, n_now)]:
+        carry = inter[(block_out + hop_no) % n_now]
+        rows.append(
+            jax.lax.ppermute(
+                carry, mesh_ax, [(to_i, (to_i + hop_no) % n_now) for to_i in range(n_now)]
+            )
+        )
+    before = jnp.stack(rows)
+    inter = before[(block_out - jnp.arange(n_now)) % n_now]
+    return settle_the_clusters(inter, vector)
 
 
 def tiled_sums(rows_in, slot_in):
@@ -35,7 +67,7 @@
     send_slots = jnp.where(is_valid, slot_ids, -1)
     got_blocks, got_slots = (
         lax.all_to_all(send_blocks, "mem", split_axis=0, concat_axis=0, tiled=True),
-        lax.all_to_all(send_slots, "mem", split_axis=0, concat_axis=0, tiled=True),
+        _shape_body(send_slots, "mem", 0, 0),
     )
     rows_in = got_blocks.reshape(members * capacity, lane_count)
     slot_in = got_slots.reshape(members * capacity)

time: 169 us -> 178 us (1.053)
  starting transfers between devices: 9.75 us -> 15.3 us
  other arithmetic: 16.2 us -> 20.2 us
  local copies, waits for them, and re-layouts: 8.35 us -> 12.3 us
  waiting for transfers between devices: 83.5 us -> 79.9 us
    ppermute x0 -> x7, starting transfers between devices: none -> 11.9 us  [_shape_body(): jax.lax.ppermute(carry, mesh_ax, [(to_i, (to_i + hop_no) % n_now) for to_...]
    all_to_all x1 -> x0, starting transfers between devices: 6.35 us -> none  [per_device(): lax.all_to_all(send_slots, 'mem', split_axis=0, concat_axis=0, tiled=True)]
    all_to_all x1, waiting for transfers between devices: 5.7 us -> 0.07 us  [per_device(): lax.all_to_all(send_blocks, 'mem', split_axis=0, concat_axis=0, tiled=True)]
    another operation x0 -> x7, other arithmetic: none -> 4.62 us
    psum x1, waiting for transfers between devices: 74.6 us -> 78.5 us  [per_device(): reduced = lax.psum(payload, 'grp')]
    another operation x0 -> x8, local copies, waits for them, and re-layouts: none -> 3.6 us
    all_to_all x1 -> x0, waiting for transfers between devices: 3.21 us -> none  [per_device(): lax.all_to_all(send_slots, 'mem', split_axis=0, concat_axis=0, tiled=True)]
  transfers between devices with their start and end apart: 3 -> 9, of which waited for: 3 -> 3; matrix products, arithmetic and copies ran while one was open for 3% -> 3% of each run, Pallas kernels for 0% -> 0%
where the time goes in v1:
time: 178 us
  waiting for transfers between devices  79.9 us (45%)
  blocking collectives  27.7 us (16%)
  other arithmetic  20.2 us (11%)
  starting transfers between devices  15.3 us (9%)
  between operations  14.2 us (8%)
  local copies, waits for them, and re-layouts  12.3 us (7%)
  matrix products  8.06 us (5%)
    psum x1, waiting for transfers between devices, per_device(): reduced = lax.psum(payload, 'grp')  78.5 us
    psum x1, blocking collectives, per_device(): reduced = lax.psum(payload, 'grp')  17.4 us
    ppermute x7, starting transfers between devices, _shape_body(): jax.lax.ppermute(carry, mesh_ax, [(to_i, (to_i + hop_no) % n_now) for to_...  11.9 us
    all_to_all x1, blocking collectives, per_device(): lax.all_to_all(back_rows, 'mem', split_axis=0, concat_axis=0, tiled=True)  10.3 us
    dot_general x7, matrix products, one_tile(): return jnp.dot(onehot, rows_in, preferred_element_type=jnp.float32)  8.06 us
    div x1, other arithmetic, per_device(): averaged = reduced[0] / jnp.maximum(total_count, 1.0)[:, None]  5.72 us
    another operation x7, other arithmetic  4.62 us
    add x7, other arithmetic, one_tile(): wanted = first + lax.broadcasted_iota(jnp.int32, (tile, 1), 0)  4.53 us
  transfers between devices with their start and end apart: 9, of which 3 were waited for; matrix products, arithmetic and copies ran while one was open for 3% of the time, Pallas kernels for 0%

profile of v1, /device:TPU:0, one launch (start us, length us, event | category | flops | bytes accessed | tf_op | source)
XLA Modules:
  0.0 177.8 jit_solution(16777742917108842576)
XLA Ops:
  7.3 0.8 bitcast_select_fusion.1
  8.6 2.6 %collective-permute-start.1 = (s32[1,32]{1,0:T(1,128)S(1)}, s32[1,32]{1,0:T(1,128)S(1)}, u32[]{:S(2)}, u32[]{:S(2)}) collective-permute-start(s32[1,32]{1,0:T(1,128)S(1)} %get-tuple-element.53), channel_id=1, source_target_pairs={{0,2},{1,3},{2,4},{3,5},{4,6},{5,7},{6,0},{7,1},{8,10},{9,11},{10,... | collective-permute-start | bytes 392 | tf_op jit(solution)/shard_map/ppermute | solution.py:33
  11.2 2.5 %collective-permute-start.2 = (s32[1,32]{1,0:T(1,128)S(1)}, s32[1,32]{1,0:T(1,128)S(1)}, u32[]{:S(2)}, u32[]{:S(2)}) collective-permute-start(s32[1,32]{1,0:T(1,128)S(1)} %get-tuple-element.52), channel_id=1, source_target_pairs={{0,3},{1,4},{2,5},{3,6},{4,7},{5,0},{6,1},{7,2},{8,11},{9,12},{10,... | collective-permute-start | bytes 392 | tf_op jit(solution)/shard_map/ppermute | solution.py:33
  13.7 1.2 collective-permute-start.3
  15.0 1.2 collective-permute-start.4
  16.2 0.7 iota_compare_fusion
  16.9 1.6 bitcast_select_fusion
  18.5 3.4 %all-to-all-start = ((bf16[8,32,128]{2,1,0:T(8,128)(2,1)}), bf16[8,32,128]{2,1,0:T(8,128)(2,1)S(1)}, u32[]{:S(2)}, u32[]{:S(2)}) async-start(bf16[8,32,128]{2,1,0:T(8,128)(2,1)} %bitcast_select_fusion), calls=%async_computation | async-start | bytes 131072 | tf_op jit(solution)/shard_map/all_to_all | solution.py:69
  21.9 3.8 %collective-permute-start.5 = (s32[1,32]{1,0:T(1,128)S(1)}, s32[1,32]{1,0:T(1,128)S(1)}, u32[]{:S(2)}, u32[]{:S(2)}) collective-permute-start(s32[1,32]{1,0:T(1,128)S(1)} %get-tuple-element.49), channel_id=1, source_target_pairs={{0,6},{1,7},{2,0},{3,1},{4,2},{5,3},{6,4},{7,5},{8,14},{9,15},{10,... | collective-permute-start | bytes 392 | tf_op jit(solution)/shard_map/ppermute | solution.py:33
  25.7 1.3 collective-permute-done.5
  27.7 25.5 %while.10 = (s32[]{:T(128)}, f32[7,1024,128]{2,1,0:T(8,128)}, s32[7]{0:T(128)S(1)}, s32[8,1,32]{2,1,0:T(1,128)S(1)}, bf16[256,128]{1,0:T(8,128)(2,1)S(1)}, /*index=5*/s32[]{:T(128)}, s32[]{:T(128)}) while((s32[]{:T(128)}, f32[7,1024,128]{2,1,0:T(8,128)}, s32[7]{0:T(128)S(1)}, s32[8,1,32]{2,1,0:T(1,128)S(1)}, bf16[256,128]{1,0:T(8,128)(2,1)S(1)}, ...), condition=%wide.region_1.2_spmd, body=%wide.region_0.1_spmd.sunk | while | flops 67372032 | bytes 603253 | solution.py:52
  30.2 1.2 fusion.16
  33.8 1.2 fusion.16
  37.5 1.1 fusion.16
  41.1 1.2 fusion.16
  44.8 1.2 fusion.16
  48.4 1.2 fusion.16
  52.0 1.2 fusion.16
  53.4 2.1 %scatter_custom_fusion = f32[7168]{0:T(1024)S(1)} fusion(s32[256]{0:T(256)S(1)} %reshape.173, f32[256]{0:T(256)S(1)} %reshape.175, f32[]{:T(128)} %constant.85.clone.1), kind=kCustom, calls=%fused_computation.13 | custom fusion | flops 256 | bytes 28676 | tf_op jit(solution)/shard_map/scatter-add | solution.py:57
  55.5 17.4 %psum.15 = f32[7168]{0:T(1024)S(1)} all-reduce(f32[7168]{0:T(1024)S(1)} %scatter_custom_fusion), channel_id=1, replica_groups=mesh['grp'=4,'mem'=8] {'grp'}, use_global_device_ids=true, to_apply=%region_4.5 | all-reduce | flops 7168 | bytes 57344 | tf_op jit(solution)/shard_map/psum | solution.py:77
  72.9 78.5 %all-reduce.2.cloned.1.call-done = f32[7168,128]{1,0:T(8,128)} async-done(((f32[7168,128]{1,0:T(8,128)}), f32[7168,128]{1,0:T(8,128)}) %all-reduce.2.cloned.1.call-update) | async-done | bytes 3670032 | tf_op jit(solution)/shard_map/psum | solution.py:77
  151.4 5.7 %broadcast_divide_fusion = f32[7168,128]{1,0:T(8,128)} fusion(f32[7168,128]{1,0:T(8,128)} %all-reduce.2.cloned.1.call-done, f32[7168]{0:T(1024)S(1)} %broadcast_maximum_fusion), kind=kLoop, calls=%fused_computation.9 | loop fusion | flops 917504 | bytes 7368704 | tf_op jit(solution)/shard_map/div | solution.py:79
  157.1 2.8 %gather_fusion.1 = bf16[256,128]{1,0:T(8,128)(2,1)S(1)} fusion(f32[7168,128]{1,0:T(8,128)} %broadcast_divide_fusion, s32[1024]{0:T(1024)S(1)} %pad_clamp_fusion), kind=kCustom, calls=%fused_computation.1 | custom fusion | bytes 132096 | tf_op jit(solution)/shard_map/jit(_take)/gather | solution.py:80
  160.0 10.3 %all_to_all.10 = bf16[8,32,128]{2,1,0:T(8,128)(2,1)S(1)} all-to-all(bf16[8,32,128]{2,1,0:T(8,128)(2,1)S(1)} %select_convert_fusion), channel_id=1, replica_groups=mesh['grp'=4,'mem'=8] {'mem'}, dimensions={0} | all-to-all | bytes 131072 | tf_op jit(solution)/shard_map/all_to_all | solution.py:83
  (61 shorter events, 19.6 us)
Async XLA Ops:
  8.0 13.9 %collective-permute-start = (s32[1,32]{1,0:T(1,128)S(1)}, s32[1,32]{1,0:T(1,128)S(1)}, u32[]{:S(2)}, u32[]{:S(2)}) collective-permute-start(s32[1,32]{1,0:T(1,128)S(1)} %get-tuple-element.54), channel_id=1, source_target_pairs={{0,1},{1,2},{2,3},{3,4},{4,5},{5,6},{6,7},{7,0},{8,9},{9,10},{10,1... | collective-permute-start | bytes 392 | tf_op jit(solution)/shard_map/ppermute | solution.py:33
  8.6 17.1 %collective-permute-start.1 = (s32[1,32]{1,0:T(1,128)S(1)}, s32[1,32]{1,0:T(1,128)S(1)}, u32[]{:S(2)}, u32[]{:S(2)}) collective-permute-start(s32[1,32]{1,0:T(1,128)S(1)} %get-tuple-element.53), channel_id=1, source_target_pairs={{0,2},{1,3},{2,4},{3,5},{4,6},{5,7},{6,0},{7,1},{8,10},{9,11},{10,... | collective-permute-start | bytes 392 | tf_op jit(solution)/shard_map/ppermute | solution.py:33
  11.2 14.5 %collective-permute-start.2 = (s32[1,32]{1,0:T(1,128)S(1)}, s32[1,32]{1,0:T(1,128)S(1)}, u32[]{:S(2)}, u32[]{:S(2)}) collective-permute-start(s32[1,32]{1,0:T(1,128)S(1)} %get-tuple-element.52), channel_id=1, source_target_pairs={{0,3},{1,4},{2,5},{3,6},{4,7},{5,0},{6,1},{7,2},{8,11},{9,12},{10,... | collective-permute-start | bytes 392 | tf_op jit(solution)/shard_map/ppermute | solution.py:33
  13.7 12.0 %collective-permute-start.3 = (s32[1,32]{1,0:T(1,128)S(1)}, s32[1,32]{1,0:T(1,128)S(1)}, u32[]{:S(2)}, u32[]{:S(2)}) collective-permute-start(s32[1,32]{1,0:T(1,128)S(1)} %get-tuple-element.51), channel_id=1, source_target_pairs={{0,4},{1,5},{2,6},{3,7},{4,0},{5,1},{6,2},{7,3},{8,12},{9,13},{10,... | collective-permute-start | bytes 392 | tf_op jit(solution)/shard_map/ppermute | solution.py:33
  15.0 10.7 %collective-permute-start.4 = (s32[1,32]{1,0:T(1,128)S(1)}, s32[1,32]{1,0:T(1,128)S(1)}, u32[]{:S(2)}, u32[]{:S(2)}) collective-permute-start(s32[1,32]{1,0:T(1,128)S(1)} %get-tuple-element.50), channel_id=1, source_target_pairs={{0,5},{1,6},{2,7},{3,0},{4,1},{5,2},{6,3},{7,4},{8,13},{9,14},{10,... | collective-permute-start | bytes 392 | tf_op jit(solution)/shard_map/ppermute | solution.py:33
  18.5 9.2 %all-to-all-start = ((bf16[8,32,128]{2,1,0:T(8,128)(2,1)}), bf16[8,32,128]{2,1,0:T(8,128)(2,1)S(1)}, u32[]{:S(2)}, u32[]{:S(2)}) async-start(bf16[8,32,128]{2,1,0:T(8,128)(2,1)} %bitcast_select_fusion), calls=%async_computation | async-start | bytes 131072 | tf_op jit(solution)/shard_map/all_to_all | solution.py:69
  21.8 129.6 %all-reduce.2.cloned.1.call-start = ((), (), s32[]{:S(2)}) async-start(), calls=%async_computation.2 | async-start | bytes 7340032 | tf_op jit(solution)/shard_map/psum | solution.py:77
  21.9 5.0 %collective-permute-start.5 = (s32[1,32]{1,0:T(1,128)S(1)}, s32[1,32]{1,0:T(1,128)S(1)}, u32[]{:S(2)}, u32[]{:S(2)}) collective-permute-start(s32[1,32]{1,0:T(1,128)S(1)} %get-tuple-element.49), channel_id=1, source_target_pairs={{0,6},{1,7},{2,0},{3,1},{4,2},{5,3},{6,4},{7,5},{8,14},{9,15},{10,... | collective-permute-start | bytes 392 | tf_op jit(solution)/shard_map/ppermute | solution.py:33
  25.7 1.3 collective-permute-start.6
Sparse Core Ops, SparseCore 0:
  53.3 98.0 all-reduce.1
